TPU v7x, 32 devices: a whole 2x2x4 slice. The times are simulated.
32 devices in a mesh: groups: 2 (over x), tensor: 16 (over z, y, core).
Axes of the slice: x: 2, y: 2, z: 4, core: 2. Of those that a mesh axis runs over, the one named last changes fastest.
Arguments:
- video_state: float32 [128, 4096], P(('groups', 'tensor')), parts along dimension 0, may hold values from -54 to 54
- audio_state: float32 [128, 2048], P(('groups', 'tensor')), parts along dimension 0, may hold values from -54 to 54
- video_modulation: float32 [12, 4096], P('groups'), parts along dimension 0, may hold values from -3 to 3
- audio_modulation: float32 [12, 2048], P('groups'), parts along dimension 0, may hold values from -3 to 3
- video_query: bfloat16 [4096, 2048], P(None, 'tensor'), may hold values from -0.09375 to 0.09375
- audio_keyval: bfloat16 [2048, 2, 2048], P(None, None, 'tensor'), may hold values from -0.125 to 0.125
- video_output: bfloat16 [2048, 4096], P('tensor'), may hold values from -0.125 to 0.125
- audio_query: bfloat16 [2048, 2048], P(None, 'tensor'), may hold values from -0.125 to 0.125
- video_keyval: bfloat16 [4096, 2, 2048], P(None, None, 'tensor'), may hold values from -0.09375 to 0.09375
- audio_output: bfloat16 [2048, 2048], P('tensor'), may hold values from -0.125 to 0.125
- video_expand: bfloat16 [4096, 16384], P(None, 'tensor'), may hold values from -0.09375 to 0.09375
- video_shrink: bfloat16 [16384, 4096], P('tensor'), may hold values from -0.046875 to 0.046875
- audio_expand: bfloat16 [2048, 8192], P(None, 'tensor'), may hold values from -0.125 to 0.125
- audio_shrink: bfloat16 [8192, 2048], P('tensor'), may hold values from -0.0625 to 0.0625
Outputs:
- video_next: float32 [128, 4096], P(('groups', 'tensor')), parts along dimension 0
- audio_next: float32 [128, 2048], P(('groups', 'tensor')), parts along dimension 0
There are 2 independent parts, one for each index of `groups`. A program takes and returns all parts, laid end to end along the dimension named above; an argument that names none is the same for every part. Nothing has to cross between parts.
All inputs are finite; a program needn't handle non-finite values.
Results may differ from a plain program's by a relative error of at most 0.0029.
Values may be sent and summed in bfloat16 or wider, within the bound.
A program may use at most 64 MiB of HBM per device.

v0:
```python
import jax
import jax.numpy as jnp
from jax import lax
from jax.sharding import PartitionSpec as P

HEAD_DIM = 64
epsilon = 1e-06


def partner(block, axis, distance):
    count = lax.axis_size(axis)
    route = []
    for low in range(count):
        high = low | 1 << distance
        if high != low and high < count:
            route += [(low, high), (high, low)]
    return lax.ppermute(block, axis, route)


def modulate(states, modulation, first):
    normed = states * lax.rsqrt(jnp.mean(states * states, axis=-1, keepdims=True) + epsilon)
    return (normed * (1.0 + modulation[first + 1]) + modulation[first]).astype(jnp.bfloat16)


def head_normalize(tensor):
    values = tensor.astype(jnp.float32)
    return (values * lax.rsqrt(jnp.mean(values * values, axis=-1, keepdims=True) + epsilon)).astype(
        jnp.bfloat16
    )


def softmax_weights(scores):
    expo = jnp.exp(scores)
    return (expo / jnp.sum(expo, axis=-1, keepdims=True)).astype(jnp.bfloat16)


def local_heads(queries, key_part, value_part):
    query_count, width = queries.shape
    source_count = key_part.shape[0]
    head_count = width // HEAD_DIM
    query_hat = head_normalize(queries.reshape(query_count, head_count, HEAD_DIM))
    key_hat = head_normalize(key_part.reshape(source_count, head_count, HEAD_DIM))
    scores = jnp.einsum(
        "qhd,khd->hqk", query_hat, key_hat, preferred_element_type=jnp.float32
    ) * HEAD_DIM ** (-0.5)
    weights = softmax_weights(scores)
    values = value_part.reshape(source_count, head_count, HEAD_DIM)
    mixed = jnp.einsum("hqk,khd->qhd", weights, values, preferred_element_type=jnp.float32)
    return mixed.astype(jnp.bfloat16).reshape(query_count, width)


def project_attend(query_rows, source_rows, query_weight, keyval_weight):
    width = query_weight.shape[1]
    queries = jnp.dot(query_rows, query_weight, preferred_element_type=jnp.float32).astype(
        jnp.bfloat16
    )
    flat_weight = keyval_weight.reshape(keyval_weight.shape[0], 2 * width)
    keyvals = jnp.dot(source_rows, flat_weight, preferred_element_type=jnp.float32).astype(
        jnp.bfloat16
    )
    key_part = keyvals[:, :width]
    value_part = keyvals[:, width:]
    if width >= HEAD_DIM:
        return local_heads(queries, key_part, value_part)
    query_float = queries.astype(jnp.float32)
    key_float = key_part.astype(jnp.float32)
    query_square = jnp.sum(query_float * query_float, axis=1, keepdims=True)
    key_square = jnp.sum(key_float * key_float, axis=1, keepdims=True)
    other_query, other_key = partner((query_square, key_square), "tensor", 0)
    query_hat = (query_float * lax.rsqrt((query_square + other_query) / HEAD_DIM + epsilon)).astype(
        jnp.bfloat16
    )
    key_hat = (key_float * lax.rsqrt((key_square + other_key) / HEAD_DIM + epsilon)).astype(
        jnp.bfloat16
    )
    partial_scores = jnp.einsum("qd,kd->qk", query_hat, key_hat, preferred_element_type=jnp.float32)
    other_scores = partner(partial_scores, "tensor", 0)
    scores = (partial_scores + other_scores) * HEAD_DIM ** (-0.5)
    weights = softmax_weights(scores)
    return jnp.dot(weights, value_part, preferred_element_type=jnp.float32).astype(jnp.bfloat16)


def output_rows(mixed, weight):
    return jnp.dot(mixed, weight, preferred_element_type=jnp.float32)


def feed_rows(inputs, expand, shrink):
    hidden = jnp.dot(inputs, expand, preferred_element_type=jnp.float32)
    hidden = jax.nn.gelu(hidden, approximate=True).astype(jnp.bfloat16)
    return jnp.dot(hidden, shrink, preferred_element_type=jnp.float32)


def on_device(
    video_state,
    audio_state,
    video_modulation,
    audio_modulation,
    video_query,
    audio_keyval,
    video_output,
    audio_query,
    video_keyval,
    audio_output,
    video_expand,
    video_shrink,
    audio_expand,
    audio_shrink,
):
    video_count = video_state.shape[0]
    audio_own = modulate(audio_state, audio_modulation, 0)
    video_whole = lax.all_gather(video_state, "tensor", axis=0, tiled=True)
    video_normed = modulate(video_whole, video_modulation, 0)
    audio_normed = lax.all_gather(audio_own, "tensor", axis=0, tiled=True)
    video_mixed = project_attend(video_normed, audio_normed, video_query, audio_keyval)
    audio_mixed = project_attend(audio_normed, video_normed, audio_query, video_keyval)
    audio_term = lax.psum_scatter(
        output_rows(audio_mixed, audio_output), "tensor", scatter_dimension=0, tiled=True
    )
    audio_mid = audio_state + audio_modulation[2] * audio_term
    audio_inner_own = modulate(audio_mid, audio_modulation, 3)
    partial_term = jnp.dot(video_mixed, video_output, preferred_element_type=jnp.float32)
    full_term = lax.psum(partial_term, "tensor")
    video_mid_whole = video_whole + video_modulation[2] * full_term
    video_inner = modulate(video_mid_whole, video_modulation, 3)
    first_row = lax.axis_index("tensor") * video_count
    video_mid = lax.dynamic_slice_in_dim(video_mid_whole, first_row, video_count, 0)
    audio_inner = lax.all_gather(audio_inner_own, "tensor", axis=0, tiled=True)
    video_feed = lax.psum_scatter(
        feed_rows(video_inner, video_expand, video_shrink),
        "tensor",
        scatter_dimension=0,
        tiled=True,
    )
    audio_feed = lax.psum_scatter(
        feed_rows(audio_inner, audio_expand, audio_shrink),
        "tensor",
        scatter_dimension=0,
        tiled=True,
    )
    video_next = video_mid + video_modulation[5] * video_feed
    audio_next = audio_mid + audio_modulation[5] * audio_feed
    return (video_next, audio_next)


def solution(mesh):
    placed = (
        P(("groups", "tensor"), None),
        P(("groups", "tensor"), None),
        P("groups", None),
        P("groups", None),
        P(None, "tensor"),
        P(None, None, "tensor"),
        P("tensor", None),
        P(None, "tensor"),
        P(None, None, "tensor"),
        P("tensor", None),
        P(None, "tensor"),
        P("tensor", None),
        P(None, "tensor"),
        P("tensor", None),
    )
    return jax.shard_map(
        on_device,
        mesh=mesh,
        in_specs=placed,
        out_specs=(P(("groups", "tensor"), None), P(("groups", "tensor"), None)),
        check_vma=False,
    )
```

profile of v0, /device:TPU:0, one launch (start us, length us, event | category | flops | bytes accessed | tf_op | source)
XLA Modules:
  0.0 302.8 jit_solution(14228679446785322309)
XLA Ops:
  7.2 0.0 all-gather.5.cloned.1.call-start
  7.2 0.7 all-gather.5.cloned.1.call-update
  7.9 0.0 all-reduce.10.cloned.1.call-start
  8.0 1.8 fusion.80
  9.7 0.9 multiply_reduce_fusion.7
  10.6 0.8 fusion.54
  11.5 24.0 %all-gather.1 = bf16[16,4,2048]{2,1,0:T(4,128)(2,1)S(1)} all-gather(bf16[1,4,2048]{2,1,0:T(4,128)(2,1)S(1)} %fusion.54), channel_id=1, replica_groups=mesh['groups'=2,'tensor'=16] {'tensor'}, dimensions={0}, use_global_device_ids=true | all-gather | bytes 278528 | tf_op jit(solution)/shard_map/all_gather | solution.py:113
  35.5 0.1 reshape.113
  35.5 1.3 fusion.9
  36.8 0.1 reshape.108
  36.9 1.5 convolution_convert_fusion.2
  38.5 0.1 reshape.107
  38.6 0.7 copy.50
  39.3 0.1 multiply_reduce_fusion.3
  39.4 0.1 multiply_reduce_fusion.4
  39.6 0.7 fusion.79
  40.3 10.6 %all-gather.5.cloned.1.call-done = f32[16,4,4096]{2,1,0:T(4,128)} async-done(((f32[1,4,4096]{2,1,0:T(4,128)}), f32[16,4,4096]{2,1,0:T(4,128)}) %all-gather.5.cloned.1.call-update) | async-done | bytes 1048592 | tf_op jit(solution)/shard_map/all_gather | solution.py:111
  50.9 1.6 reshape.111
  52.5 0.2 multiply_reduce_fusion.1
  52.7 2.1 fusion.5
  54.9 0.1 reshape.109
  55.0 0.1 multiply_reduce_fusion.2
  55.2 0.7 copy.51
  55.9 1.6 fusion.8
  57.5 0.1 reshape.106
  57.6 0.1 multiply_reduce_fusion.5
  57.8 0.2 multiply_convert_fusion
  58.0 0.1 fusion.3
  58.1 0.9 convolution_convert_fusion
  59.0 2.1 fusion.84
  61.2 0.2 multiply_convert_fusion.2
  61.4 0.1 fusion.4
  61.6 0.9 convolution_convert_fusion.1
  62.5 2.6 fusion.83
  65.1 0.0 all-reduce.10.cloned.1.call-update
  65.1 0.0 all-reduce.8.cloned.1.call-start
  65.2 0.6 dynamic-slice
  66.4 93.9 %all-reduce.10.cloned.1.call-done = (f32[64,4096]{1,0:T(8,128)}, f32[64,2048]{1,0:T(8,128)}) async-done(((f32[64,4096]{1,0:T(8,128)}, f32[64,2048]{1,0:T(8,128)}), (f32[64,4096]{1,0:T(8,128)}, f32[64,2048]{1,0:T(8,128)})) %all-reduce.10.cloned.1.call-update) | async-done | bytes 1572880 | tf_op jit(solution)/shard_map/psum | solution.py:122
  160.3 1.0 multiply_reduce_fusion.6
  161.3 0.1 fusion.55
  161.4 21.4 %all-gather.2 = bf16[16,4,2048]{2,1,0:T(4,128)(2,1)} all-gather(bf16[1,4,2048]{2,1,0:T(4,128)(2,1)S(1)} %fusion.55), channel_id=1, replica_groups=mesh['groups'=2,'tensor'=16] {'tensor'}, dimensions={0}, use_global_device_ids=true | all-gather | bytes 278528 | tf_op jit(solution)/shard_map/all_gather | solution.py:127
  182.8 1.0 reshape.115
  183.8 2.5 multiply_reduce_fusion
  186.4 3.4 %fusion.37 = f32[64,2048]{1,0:T(8,128)} fusion(bf16[512,2048]{1,0:T(8,128)(2,1)S(1)} %copy-done, bf16[64,2048]{1,0:T(8,128)(2,1)S(1)} %reshape.115, bf16[2048,512]{1,0:T(8,128)(2,1)} %param.26), kind=kOutput, calls=%fused_computation.49 | convolution fusion | flops 268730368 | bytes 4980736 | tf_op jit(solution)/shard_map/dot_general | solution.py:90
  189.8 9.9 %fusion.24 = f32[64,4096]{1,0:T(8,128)} fusion(bf16[1024,4096]{1,0:T(8,128)(2,1)} %param.25, bf16[4096,1024]{1,0:T(8,128)(2,1)} %param.24, f32[64,4096]{1,0:T(8,128)S(1)} %copy-done.1, f32[4096]{0:T(1024)S(1)} %bitcast.60, f32[4096]{0:T(1024)S(1)} %bitcast.61, f32[64]{0:T(128)S(1)} %add_rsqrt_fusion.5), kind=kOutput, calls=%fused_computation.35 | convolution fusion | flops 1075380224 | bytes 18907392 | tf_op jit(solution)/shard_map/dot_general | solution.py:90
  199.8 93.4 %all-reduce.8.cloned.1.call-done = (f32[64,4096]{1,0:T(8,128)}, f32[64,2048]{1,0:T(8,128)}) async-done(((f32[64,4096]{1,0:T(8,128)}, f32[64,2048]{1,0:T(8,128)}), (f32[64,4096]{1,0:T(8,128)}, f32[64,2048]{1,0:T(8,128)})) %all-reduce.8.cloned.1.call-update) | async-done | bytes 1572880
  293.2 1.5 fusion.44
  294.7 1.6 fusion.39
  (39 shorter events, 0.2 us)
Async XLA Ops:
  7.2 179.2 %copy-start = (bf16[512,2048]{1,0:T(8,128)(2,1)S(1)}, bf16[512,2048]{1,0:T(8,128)(2,1)}, u32[]{:S(2)}) copy-start(bf16[512,2048]{1,0:T(8,128)(2,1)} %param.27) | copy-start | bytes 6291460
  7.2 32.4 %copy-start.3 = (f32[6,4096]{1,0:T(8,128)S(1)}, f32[6,4096]{1,0:T(8,128)}, u32[]{:S(2)}) copy-start(f32[6,4096]{1,0:T(8,128)} %param.16) | copy-start | bytes 294916
  7.2 43.8 %all-gather.5.cloned.1.call-start = ((), (), s32[]{:S(2)}) async-start(), calls=%async_computation | async-start | bytes 1114112 | tf_op jit(solution)/shard_map/all_gather | solution.py:111
  7.9 152.4 %all-reduce.10.cloned.1.call-start = ((), (), s32[]{:S(2)}) async-start(), calls=%async_computation.2 | async-start | bytes 3145728 | tf_op jit(solution)/shard_map/psum | solution.py:122
  40.3 14.5 %copy-start.4 = (f32[1,4096]{1,0:T(1,128)}, f32[1,4096]{1,0:T(1,128)S(1)}, u32[]{:S(2)}) copy-start(f32[1,4096]{1,0:T(1,128)S(1)} %get-tuple-element.11) | copy-start | bytes 49156
  40.3 14.6 %copy-start.5 = (f32[1,4096]{1,0:T(1,128)}, f32[1,4096]{1,0:T(1,128)S(1)}, u32[]{:S(2)}) copy-start(f32[1,4096]{1,0:T(1,128)S(1)} %get-tuple-element.12) | copy-start | bytes 49156
  61.4 3.8 %copy-start.13 = (u32[32]{0:T(128)S(1)}, u32[32]{0:T(128)}, u32[]{:S(2)}) copy-start(u32[32]{0:T(128)} %constant.50) | copy-start | bytes 388
  61.4 99.0 %copy-start.2 = (f32[4,2048]{1,0:T(4,128)S(1)}, f32[4,2048]{1,0:T(4,128)}, u32[]{:S(2)}) copy-start(f32[4,2048]{1,0:T(4,128)} %param.15) | copy-start | bytes 98308
  61.4 98.9 %copy-start.12 = (f32[1,2048]{1,0:T(1,128)S(1)}, f32[1,2048]{1,0:T(1,128)}, u32[]{:S(2)}) copy-start(f32[1,2048]{1,0:T(1,128)} %get-tuple-element.17) | copy-start | bytes 24580
  61.5 99.8 %copy-start.10 = (f32[1,2048]{1,0:T(1,128)S(1)}, f32[1,2048]{1,0:T(1,128)}, u32[]{:S(2)}) copy-start(f32[1,2048]{1,0:T(1,128)} %get-tuple-element.20) | copy-start | bytes 24580
  61.6 99.8 %copy-start.11 = (f32[1,2048]{1,0:T(1,128)S(1)}, f32[1,2048]{1,0:T(1,128)}, u32[]{:S(2)}) copy-start(f32[1,2048]{1,0:T(1,128)} %get-tuple-element.21) | copy-start | bytes 24580
  65.1 228.1 %all-reduce.8.cloned.1.call-start = ((), (), s32[]{:S(2)}) async-start(), calls=%async_computation.1 | async-start | bytes 3145728
  186.3 3.4 %copy-start.1 = (f32[64,4096]{1,0:T(8,128)S(1)}, f32[64,4096]{1,0:T(8,128)}, u32[]{:S(2)}) copy-start(f32[64,4096]{1,0:T(8,128)} %get-tuple-element.9) | copy-start | bytes 3145732
  186.3 3.4 %copy-start.7 = (f32[1,4096]{1,0:T(1,128)S(1)}, f32[1,4096]{1,0:T(1,128)}, u32[]{:S(2)}) copy-start(f32[1,4096]{1,0:T(1,128)} %get-tuple-element.14) | copy-start | bytes 49156
  186.3 3.4 %copy-start.8 = (f32[1,4096]{1,0:T(1,128)S(1)}, f32[1,4096]{1,0:T(1,128)}, u32[]{:S(2)}) copy-start(f32[1,4096]{1,0:T(1,128)} %get-tuple-element.15) | copy-start | bytes 49156
  189.8 103.4 %copy-start.9 = (f32[1,2048]{1,0:T(1,128)S(1)}, f32[1,2048]{1,0:T(1,128)}, u32[]{:S(2)}) copy-start(f32[1,2048]{1,0:T(1,128)} %get-tuple-element.16) | copy-start | bytes 24580
  189.8 104.9 %copy-start.6 = (f32[1,4096]{1,0:T(1,128)S(1)}, f32[1,4096]{1,0:T(1,128)}, u32[]{:S(2)}) copy-start(f32[1,4096]{1,0:T(1,128)} %get-tuple-element.10) | copy-start | bytes 49156
Sparse Core Ops, SparseCore 0:
  10.2 40.7 all-gather.4
  65.2 95.0 all-reduce.9
  199.9 93.2 all-reduce.7
where the time goes:
time: 304 us; the launch traced here: 303 us
  waiting for transfers between devices  199 us (65%)
  blocking collectives  45.4 us (15%)
  matrix products  26.7 us (9%)
  between operations  14.8 us (5%)
  other arithmetic  12 us (4%)
  local copies, waits for them, and re-layouts  5.14 us (2%)
    unnamed x4, waiting for transfers between devices  94.1 us
    psum x1, waiting for transfers between devices, on_device(): full_term = lax.psum(partial_term, 'tensor')  93.9 us
    all_gather x1, blocking collectives, on_device(): audio_normed = lax.all_gather(audio_own, 'tensor', axis=0, tiled=True)  24 us
    all_gather x1, blocking collectives, on_device(): audio_inner = lax.all_gather(audio_inner_own, 'tensor', axis=0, tiled=True)  21.4 us
    dot_general x2, matrix products, feed_rows(): return jnp.dot(hidden, shrink, preferred_element_type=jnp.float32)  13.4 us
    all_gather x1, waiting for transfers between devices, on_device(): video_whole = lax.all_gather(video_state, 'tensor', axis=0, tiled=True)  10.6 us
  transfers between devices with their start and end apart: 3, of which 3 were waited for; matrix products, arithmetic and copies ran while one was open for 3% of the time, Pallas kernels for 0%

commit v1 on v0

--- a/solution.py
+++ b/solution.py
@@ -119,7 +119,7 @@
     audio_mid = audio_state + audio_modulation[2] * audio_term
     audio_inner_own = modulate(audio_mid, audio_modulation, 3)
     partial_term = jnp.dot(video_mixed, video_output, preferred_element_type=jnp.float32)
-    full_term = lax.psum(partial_term, "tensor")
+    full_term = jnp.sum(lax.all_gather(partial_term, "tensor"), axis=0)
     video_mid_whole = video_whole + video_modulation[2] * full_term
     video_inner = modulate(video_mid_whole, video_modulation, 3)
     first_row = lax.axis_index("tensor") * video_count

time: 304 us -> 406 us (1.34)
  waiting for transfers between devices: 199 us -> 292 us
  other arithmetic: 12 us -> 19.9 us
    all_gather x0 -> x1, waiting for transfers between devices: none -> 100 us  [on_device(): full_term = jnp.sum(lax.all_gather(partial_term, 'tensor'), axis=0)]
    psum x1 -> x0, waiting for transfers between devices: 93.9 us -> none  [on_device(): full_term = lax.psum(partial_term, 'tensor')]
    unnamed x4 -> x6, waiting for transfers between devices: 94.1 us -> 181 us
    reduce_sum x0 -> x1, other arithmetic: none -> 7.88 us  [on_device(): full_term = jnp.sum(lax.all_gather(partial_term, 'tensor'), axis=0)]
  transfers between devices with their start and end apart: 3 -> 4, of which waited for: 3 -> 4; matrix products, arithmetic and copies ran while one was open for 3% -> 4% of each run, Pallas kernels for 0% -> 0%
where the time goes in v1:
time: 406 us
  waiting for transfers between devices  292 us (72%)
  blocking collectives  48.1 us (12%)
  matrix products  25.1 us (6%)
  other arithmetic  19.9 us (5%)
  between operations  14.8 us (4%)
  local copies, waits for them, and re-layouts  5.14 us (1%)
    unnamed x6, waiting for transfers between devices  181 us
    all_gather x1, waiting for transfers between devices, on_device(): full_term = jnp.sum(lax.all_gather(partial_term, 'tensor'), axis=0)  100 us
    all_gather x1, blocking collectives, on_device(): audio_inner = lax.all_gather(audio_inner_own, 'tensor', axis=0, tiled=True)  24.1 us
    all_gather x1, blocking collectives, on_device(): audio_normed = lax.all_gather(audio_own, 'tensor', axis=0, tiled=True)  24 us
    dot_general x2, matrix products, feed_rows(): return jnp.dot(hidden, shrink, preferred_element_type=jnp.float32)  13.6 us
    all_gather x1, waiting for transfers between devices, on_device(): video_whole = lax.all_gather(video_state, 'tensor', axis=0, tiled=True)  11.6 us
  transfers between devices with their start and end apart: 4, of which 4 were waited for; matrix products, arithmetic and copies ran while one was open for 4% of the time, Pallas kernels for 0%

profile of v1, /device:TPU:0, one launch (start us, length us, event | category | flops | bytes accessed | tf_op | source)
XLA Modules:
  0.0 405.7 jit_solution(4449643512973796201)
XLA Ops:
  7.2 0.7 all-gather.9.cloned.1.call-update
  8.0 1.8 fusion.80
  9.7 0.9 multiply_reduce_fusion.7
  10.6 0.8 fusion.54
  11.5 24.0 %all-gather.2 = bf16[16,4,2048]{2,1,0:T(4,128)(2,1)S(1)} all-gather(bf16[1,4,2048]{2,1,0:T(4,128)(2,1)S(1)} %fusion.54), channel_id=1, replica_groups=mesh['groups'=2,'tensor'=16] {'tensor'}, dimensions={0}, use_global_device_ids=true | all-gather | bytes 278528 | tf_op jit(solution)/shard_map/all_gather | solution.py:113
  35.5 0.1 reshape.114
  35.5 1.6 convolution_convert_fusion.2
  37.1 0.7 copy.50
  37.8 0.1 reshape.107
  38.0 0.2 fusion.9
  38.2 0.1 reshape.108
  38.3 0.1 multiply_reduce_fusion.4
  38.4 0.1 multiply_reduce_fusion.3
  38.6 0.7 fusion.79
  39.3 11.6 %all-gather.9.cloned.1.call-done = f32[16,4,4096]{2,1,0:T(4,128)} async-done(((f32[1,4,4096]{2,1,0:T(4,128)}), f32[16,4,4096]{2,1,0:T(4,128)}) %all-gather.9.cloned.1.call-update) | async-done | bytes 1048592 | tf_op jit(solution)/shard_map/all_gather | solution.py:111
  50.9 1.6 reshape.112
  52.5 0.2 multiply_reduce_fusion.1
  52.7 1.6 fusion.8
  54.3 0.1 reshape.106
  54.4 0.1 multiply_reduce_fusion.5
  54.6 2.1 fusion.5
  56.7 0.7 copy.51
  57.4 0.1 reshape.109
  57.5 0.1 multiply_reduce_fusion.2
  57.7 0.2 multiply_convert_fusion
  57.9 0.1 fusion.3
  58.1 0.9 convolution_convert_fusion
  59.0 2.1 fusion.84
  61.2 0.0 all-gather.7.cloned.1.call-start
  61.2 0.2 multiply_convert_fusion.2
  61.4 0.1 fusion.4
  61.6 0.1 convolution_convert_fusion.1
  61.7 2.6 fusion.83
  64.3 0.0 all-reduce.9.cloned.1.call-start
  64.4 0.6 dynamic-slice
  65.6 85.5 %all-reduce.7.cloned.1.call-done = f32[64,2048]{1,0:T(8,128)} async-done(((f32[64,2048]{1,0:T(8,128)}), f32[64,2048]{1,0:T(8,128)}) %all-reduce.7.cloned.1.call-update) | async-done | bytes 524304
  151.2 1.0 multiply_reduce_fusion.6
  152.2 0.1 fusion.55
  152.2 24.1 %all-gather.3 = bf16[16,4,2048]{2,1,0:T(4,128)(2,1)} all-gather(bf16[1,4,2048]{2,1,0:T(4,128)(2,1)S(1)} %fusion.55), channel_id=1, replica_groups=mesh['groups'=2,'tensor'=16] {'tensor'}, dimensions={0}, use_global_device_ids=true | all-gather | bytes 278528 | tf_op jit(solution)/shard_map/all_gather | solution.py:127
  176.3 1.0 reshape.116
  177.4 3.4 fusion.37
  180.7 100.1 %all-gather.7.cloned.1.call-done = f32[1024,4096]{1,0:T(8,128)} async-done(((f32[64,4096]{1,0:T(8,128)}), f32[1024,4096]{1,0:T(8,128)}) %all-gather.7.cloned.1.call-update) | async-done | bytes 16777232 | tf_op jit(solution)/shard_map/all_gather | solution.py:122
  280.9 7.9 %reduce_sum.104 = f32[64,4096]{1,0:T(8,128)} reduce(f32[16,64,4096]{2,1,0:T(8,128)} %bitcast.54, f32[]{:T(128)} %constant.14.clone.1), dimensions={0}, to_apply=%region_5.0 | reduce | flops 3932160 | bytes 17825796 | tf_op jit(solution)/shard_map/reduce_sum | solution.py:122
  288.7 2.5 multiply_reduce_fusion
  291.3 10.2 %fusion.24 = f32[64,4096]{1,0:T(8,128)} fusion(bf16[1024,4096]{1,0:T(8,128)(2,1)} %param.25, bf16[4096,1024]{1,0:T(8,128)(2,1)} %param.24, f32[64,4096]{1,0:T(8,128)} %get-tuple-element.7, f32[4096]{0:T(1024)S(1)} %bitcast.62, f32[4096]{0:T(1024)S(1)} %bitcast.63, f32[64]{0:T(128)S(1)} %add_rsqrt_fusion.5), kind=kOutput, calls=%fused_computation.35 | convolution fusion | flops 1075380224 | bytes 18907392 | tf_op jit(solution)/shard_map/dot_general | solution.py:90
  301.6 94.5 %all-reduce.9.cloned.1.call-done = (f32[64,4096]{1,0:T(8,128)}, f32[64,2048]{1,0:T(8,128)}) async-done(((f32[64,4096]{1,0:T(8,128)}, f32[64,2048]{1,0:T(8,128)}), (f32[64,4096]{1,0:T(8,128)}, f32[64,2048]{1,0:T(8,128)})) %all-reduce.9.cloned.1.call-update) | async-done | bytes 1572880
  396.0 1.5 fusion.44
  397.5 1.6 fusion.39
  (41 shorter events, 0.3 us)
Async XLA Ops:
  7.2 170.2 %copy-start = (bf16[512,2048]{1,0:T(8,128)(2,1)S(1)}, bf16[512,2048]{1,0:T(8,128)(2,1)}, u32[]{:S(2)}) copy-start(bf16[512,2048]{1,0:T(8,128)(2,1)} %param.27) | copy-start | bytes 6291460
  7.2 30.8 %copy-start.1 = (bf16[2048,128]{1,0:T(8,128)(2,1)S(1)}, bf16[2048,128]{1,0:T(8,128)(2,1)}, u32[]{:S(2)}) copy-start(bf16[2048,128]{1,0:T(8,128)(2,1)} %param.21) | copy-start | bytes 1572868
  7.2 43.8 %all-gather.9.cloned.1.call-start = ((), (), s32[]{:S(2)}) async-start(), calls=%async_computation.1 | async-start | bytes 1114112 | tf_op jit(solution)/shard_map/all_gather | solution.py:111
  7.9 143.2 %all-reduce.7.cloned.1.call-start = ((), (), s32[]{:S(2)}) async-start(), calls=%async_computation.2 | async-start | bytes 1048576
  35.5 3.1 copy-start.3
  57.9 3.7 copy-start.7
  61.1 3.3 copy-start.12
  61.1 90.0 %copy-start.2 = (f32[4,2048]{1,0:T(4,128)S(1)}, f32[4,2048]{1,0:T(4,128)}, u32[]{:S(2)}) copy-start(f32[4,2048]{1,0:T(4,128)} %param.15) | copy-start | bytes 98308
  61.1 90.0 %copy-start.11 = (f32[1,2048]{1,0:T(1,128)S(1)}, f32[1,2048]{1,0:T(1,128)}, u32[]{:S(2)}) copy-start(f32[1,2048]{1,0:T(1,128)} %get-tuple-element.15) | copy-start | bytes 24580
  61.2 91.0 %copy-start.9 = (f32[1,2048]{1,0:T(1,128)S(1)}, f32[1,2048]{1,0:T(1,128)}, u32[]{:S(2)}) copy-start(f32[1,2048]{1,0:T(1,128)} %get-tuple-element.18) | copy-start | bytes 24580
  61.2 91.0 %copy-start.10 = (f32[1,2048]{1,0:T(1,128)S(1)}, f32[1,2048]{1,0:T(1,128)}, u32[]{:S(2)}) copy-start(f32[1,2048]{1,0:T(1,128)} %get-tuple-element.19) | copy-start | bytes 24580
  61.2 219.7 %all-gather.7.cloned.1.call-start = ((), (), s32[]{:S(2)}) async-start(), calls=%async_computation | async-start | bytes 17825792 | tf_op jit(solution)/shard_map/all_gather | solution.py:122
  64.3 331.7 %all-reduce.9.cloned.1.call-start = ((), (), s32[]{:S(2)}) async-start(), calls=%async_computation.3 | async-start | bytes 3145728
  288.7 2.5 copy-start.5
  288.7 2.5 copy-start.6
  291.3 104.8 %copy-start.8 = (f32[1,2048]{1,0:T(1,128)S(1)}, f32[1,2048]{1,0:T(1,128)}, u32[]{:S(2)}) copy-start(f32[1,2048]{1,0:T(1,128)} %get-tuple-element.14) | copy-start | bytes 24580
  291.3 106.2 %copy-start.4 = (f32[1,4096]{1,0:T(1,128)S(1)}, f32[1,4096]{1,0:T(1,128)}, u32[]{:S(2)}) copy-start(f32[1,4096]{1,0:T(1,128)} %get-tuple-element.8) | copy-start | bytes 49156
Sparse Core Ops, SparseCore 0:
  10.2 40.7 all-gather.8
  61.3 89.8 all-reduce.6
  153.3 127.4 all-gather.6
  301.7 94.3 all-reduce.8
